TPU v7x, 32 devices: a whole 2x2x4 slice. The times are simulated.
32 devices in a mesh: ep: 4 (over y, x), fsdp: 8 (over z, core).
Axes of the slice: x: 2, y: 2, z: 4, core: 2. Of those that a mesh axis runs over, the one named last changes fastest.
Arguments:
- train_gate: float32 [64, 2048, 1408], P('ep', 'fsdp'), may hold values from -0.1875 to 0.1875
- train_up: float32 [64, 2048, 1408], P('ep', 'fsdp'), may hold values from -0.1875 to 0.1875
- train_down: float32 [64, 1408, 2048], P('ep', None, 'fsdp'), may hold values from -0.21875 to 0.21875
- router_weight: float32 [2048, 64], P('fsdp', 'ep'), may hold values from -0.125 to 0.125
- router_gain: float32 [2048], P('fsdp'), may hold values from 0.25 to 1.75
Outputs:
- ready_gate: bfloat16 [64, 2048, 1408], P('ep', None, 'fsdp')
- ready_up: bfloat16 [64, 2048, 1408], P('ep', None, 'fsdp')
- ready_down: bfloat16 [64, 1408, 2048], P('ep', 'fsdp')
- scale_gate: float32 [64, 1408], P('ep', 'fsdp')
- scale_up: float32 [64, 1408], P('ep', 'fsdp')
- scale_down: float32 [64, 1408], P('ep', 'fsdp')
- serve_router: bfloat16 [2048, 64], replicated
All inputs are finite; a program needn't handle non-finite values. Where the computation divides by a largest or mean magnitude, that divisor is 1e-20 or more.
Results may differ from a plain program's by a relative error of at most 0.001.
Values may be sent and summed in bfloat16 or wider, within the bound.
A program may use at most 256 MiB of HBM per device.

v0:
```python
import jax
import jax.numpy as jnp
from jax import lax
from jax.sharding import PartitionSpec as P


def per_device(train_gate, train_up, train_down, router_weight, router_gain):
    scale_gate, scale_up, scale_down = lax.pmax(
        (
            jnp.max(jnp.abs(train_gate), axis=1),
            jnp.max(jnp.abs(train_up), axis=1),
            jnp.max(jnp.abs(train_down), axis=2),
        ),
        "fsdp",
    )
    narrow_gate, narrow_up, narrow_down = (
        (train_gate / jnp.expand_dims(scale_gate, 1)).astype(jnp.bfloat16),
        (train_up / jnp.expand_dims(scale_up, 1)).astype(jnp.bfloat16),
        (train_down / jnp.expand_dims(scale_down, 2)).astype(jnp.bfloat16),
    )
    ready_gate, ready_up = (
        lax.all_to_all(narrow_gate, "fsdp", split_axis=2, concat_axis=1, tiled=True),
        lax.all_to_all(narrow_up, "fsdp", split_axis=2, concat_axis=1, tiled=True),
    )
    ready_down = lax.all_to_all(narrow_down, "fsdp", split_axis=1, concat_axis=2, tiled=True)
    scale_gate = lax.dynamic_slice_in_dim(
        scale_gate, lax.axis_index("fsdp") * ready_gate.shape[2], ready_gate.shape[2], axis=1
    )
    scale_up = lax.dynamic_slice_in_dim(
        scale_up, lax.axis_index("fsdp") * ready_up.shape[2], ready_up.shape[2], axis=1
    )
    scale_down = lax.dynamic_slice_in_dim(
        scale_down, lax.axis_index("fsdp") * ready_down.shape[1], ready_down.shape[1], axis=1
    )
    part_router = (router_weight * router_gain[:, None]).astype(jnp.bfloat16)
    row_router = lax.all_gather(part_router, "fsdp", axis=0, tiled=True)
    serve_router = lax.all_gather(row_router, "ep", axis=1, tiled=True)
    return (ready_gate, ready_up, ready_down, scale_gate, scale_up, scale_down, serve_router)


def solution(mesh):
    placed = (
        P("ep", "fsdp", None),
        P("ep", "fsdp", None),
        P("ep", None, "fsdp"),
        P("fsdp", "ep"),
        P("fsdp"),
    )
    return jax.shard_map(
        per_device,
        mesh=mesh,
        in_specs=placed,
        out_specs=(
            P("ep", None, "fsdp"),
            P("ep", None, "fsdp"),
            P("ep", "fsdp", None),
            P("ep", "fsdp"),
            P("ep", "fsdp"),
            P("ep", "fsdp"),
            P(),
        ),
        check_vma=False,
    )
```

profile of v0, /device:TPU:0, one launch (start us, length us, event | category | flops | bytes accessed | tf_op | source)
XLA Modules:
  0.0 985.2 jit_solution(7565016768209817902)
XLA Ops:
  7.2 10.5 %abs_reduce_fusion = f32[16,1408]{1,0:T(8,128)} fusion(f32[16,1408,256]{2,1,0:T(8,128)} %param.7), kind=kLoop, calls=%fused_computation.2 | loop fusion | flops 11511808 | bytes 23158784 | tf_op jit(solution)/shard_map/reduce_max | solution.py:12
  17.7 10.8 %abs_reduce_fusion.1 = f32[16,1408]{1,0:T(8,128)} fusion(f32[16,256,1408]{2,1,0:T(8,128)} %param.6), kind=kLoop, calls=%fused_computation.4 | loop fusion | flops 11511808 | bytes 23158784 | tf_op jit(solution)/shard_map/reduce_max | solution.py:11
  28.6 2.4 abs_reduce_fusion.2
  31.0 23.7 %copy.24 = f32[16,256,1408]{1,0,2:T(8,128)} copy(f32[16,256,1408]{2,1,0:T(8,128)} %param.5) | data formatting | bytes 46137344 | tf_op args[0]
  54.7 32.5 %all-reduce.3.cloned.1.call-done = (f32[16,1408]{1,0:T(8,128)}, f32[16,1408]{1,0:T(8,128)}, f32[16,1408]{1,0:T(8,128)}) async-done(((f32[16,1408]{1,0:T(8,128)}, f32[16,1408]{1,0:T(8,128)}, f32[16,1408]{1,0:T(8,128)}), (f32[16,1408]{1,0:T(8,128)}, f32[16,1408]{1,0:T(8,128)}, f32[16,1408]{1,0:T(8,128)})) %all-reduce.3.cloned.1.call-update) | async-done | bytes 270352 | tf_op jit(solution)/shard_map/pmax | solution.py:8
  87.2 1.1 copy.23
  88.4 14.2 %divide_convert_fusion.1 = bf16[16,256,1408]{1,0,2:T(8,128)(2,1)} fusion(f32[16,256,1408]{1,0,2:T(8,128)} %copy.24, f32[16,1408]{0,1:T(8,128)S(1)} %copy.23), kind=kLoop, calls=%fused_computation.5 | loop fusion | flops 11534336 | bytes 34693120 | tf_op jit(solution)/shard_map/convert_element_type | solution.py:17
  102.6 5.4 all-to-all-start
  108.0 23.7 %copy.28 = f32[16,256,1408]{1,0,2:T(8,128)} copy(f32[16,256,1408]{2,1,0:T(8,128)} %param.6) | data formatting | bytes 46137344 | tf_op args[1]
  132.0 14.2 %divide_convert_fusion = bf16[16,256,1408]{1,0,2:T(8,128)(2,1)} fusion(f32[16,256,1408]{1,0,2:T(8,128)} %copy.28, f32[16,1408]{0,1:T(8,128)S(1)} %copy.27), kind=kLoop, calls=%fused_computation.3 | loop fusion | flops 11534336 | bytes 34693120 | tf_op jit(solution)/shard_map/convert_element_type | solution.py:18
  146.2 213.1 %all-to-all-done = bf16[16,256,1408]{1,0,2:T(8,128)(2,1)} async-done(((bf16[16,256,1408]{1,0,2:T(8,128)(2,1)}), bf16[16,256,1408]{1,0,2:T(8,128)(2,1)}, u32[]{:S(2)}, u32[]{:S(2)}) %all-to-all-start) | async-done | bytes 11534368 | tf_op jit(solution)/shard_map/all_to_all | solution.py:22
  359.4 5.2 all-to-all-start.1
  364.9 32.6 %fusion = bf16[16,1408,256]{2,0,1:T(8,128)(2,1)} fusion(f32[16,1408,256]{2,1,0:T(8,128)} %param.7, f32[16,1408]{0,1:T(8,128)S(1)} %copy.31), kind=kLoop, calls=%fused_computation.1 | loop fusion | flops 11534336 | bytes 34693120 | tf_op jit(solution)/shard_map/convert_element_type | solution.py:19
  397.5 218.4 %all-to-all-done.1 = bf16[16,256,1408]{1,0,2:T(8,128)(2,1)} async-done(((bf16[16,256,1408]{1,0,2:T(8,128)(2,1)}), bf16[16,256,1408]{1,0,2:T(8,128)(2,1)}, u32[]{:S(2)}, u32[]{:S(2)}) %all-to-all-start.1) | async-done | bytes 11534368 | tf_op jit(solution)/shard_map/all_to_all | solution.py:23
  615.9 5.3 all-to-all-start.2
  621.3 257.3 %all_gather.6 = bf16[2048,16]{0,1:T(8,128)(2,1)S(1)} all-gather(bf16[256,16]{0,1:T(8,128)(2,1)S(1)} %multiply_convert_fusion), channel_id=1, replica_groups=mesh['ep'=4,'fsdp'=8] {'fsdp'}, dimensions={0}, use_global_device_ids=true | all-gather | bytes 73728 | tf_op jit(solution)/shard_map/all_gather | solution.py:36
  878.5 9.1 all_gather.7
  887.7 1.4 constant_dynamic-slice_fusion.2
  889.8 11.3 %copy.26 = bf16[16,8,256,176]{2,1,3,0:T(8,128)(2,1)} copy(bf16[16,8,256,176]{2,0,3,1:T(8,128)(2,1)} %bitcast.2) | data formatting | bytes 23068672 | tf_op jit(solution)/shard_map/all_to_all | solution.py:22
  901.1 18.0 %all_to_all.42 = bf16[16,2048,176]{1,2,0:T(8,128)(2,1)} reshape(bf16[16,8,256,176]{2,1,3,0:T(8,128)(2,1)} %copy.26) | data formatting | bytes 23068672 | tf_op jit(solution)/shard_map/all_to_all | solution.py:22
  919.1 11.3 %copy.30 = bf16[16,8,256,176]{2,1,3,0:T(8,128)(2,1)} copy(bf16[16,8,256,176]{2,0,3,1:T(8,128)(2,1)} %bitcast.5) | data formatting | bytes 23068672 | tf_op jit(solution)/shard_map/all_to_all | solution.py:23
  930.4 18.0 %all_to_all.46 = bf16[16,2048,176]{1,2,0:T(8,128)(2,1)} reshape(bf16[16,8,256,176]{2,1,3,0:T(8,128)(2,1)} %copy.30) | data formatting | bytes 23068672 | tf_op jit(solution)/shard_map/all_to_all | solution.py:23
  948.4 11.4 %copy.33 = bf16[16,176,8,256]{3,2,1,0:T(8,128)(2,1)} copy(bf16[16,176,8,256]{3,0,1,2:T(8,128)(2,1)} %bitcast.7) | data formatting | bytes 23068672 | tf_op jit(solution)/shard_map/all_to_all | solution.py:25
  959.7 18.0 %all_to_all.50 = bf16[16,176,2048]{2,1,0:T(8,128)(2,1)} reshape(bf16[16,176,8,256]{3,2,1,0:T(8,128)(2,1)} %copy.33) | data formatting | bytes 23068672 | tf_op jit(solution)/shard_map/all_to_all | solution.py:25
  (29 shorter events, 2.0 us)
Async XLA Ops:
  7.2 80.1 %all-reduce.3.cloned.1.call-start = ((), (), s32[]{:S(2)}) async-start(), calls=%async_computation.3 | async-start | bytes 540672 | tf_op jit(solution)/shard_map/pmax | solution.py:8
  7.2 21.3 %slice-start = ((s8[23068672]{0:T(1024)(128)(4,1)}), s8[4194304]{0:T(1024)(128)(4,1)S(1)}, s32[]{:S(2)}) async-start(s8[23068672]{0:T(1024)(128)(4,1)} %bitcast.19), calls=%async_computation.4 | async-start | bytes 8388608
  7.2 21.3 %slice-start.1 = ((s8[23068672]{0:T(1024)(128)(4,1)}), s8[4194304]{0:T(1024)(128)(4,1)S(1)}, s32[]{:S(2)}) async-start(s8[23068672]{0:T(1024)(128)(4,1)} %bitcast.19), calls=%async_computation.5 | async-start | bytes 8388608
  7.2 21.3 %slice-start.2 = ((s8[23068672]{0:T(1024)(128)(4,1)}), s8[4194304]{0:T(1024)(128)(4,1)S(1)}, s32[]{:S(2)}) async-start(s8[23068672]{0:T(1024)(128)(4,1)} %bitcast.19), calls=%async_computation.6 | async-start | bytes 8388608
  17.7 10.8 %slice-start.3 = ((s8[23068672]{0:T(1024)(128)(4,1)}), s8[4194304]{0:T(1024)(128)(4,1)S(1)}, s32[]{:S(2)}) async-start(s8[23068672]{0:T(1024)(128)(4,1)} %bitcast.19), calls=%async_computation.7 | async-start | bytes 8388608
  17.7 10.8 %slice-start.4 = ((s8[23068672]{0:T(1024)(128)(4,1)}), s8[4194304]{0:T(1024)(128)(4,1)S(1)}, s32[]{:S(2)}) async-start(s8[23068672]{0:T(1024)(128)(4,1)} %bitcast.19), calls=%async_computation.8 | async-start | bytes 8388608
  17.7 10.9 %slice-start.5 = ((s8[23068672]{0:T(1024)(128)(4,1)}), s8[2097152]{0:T(1024)(128)(4,1)S(1)}, s32[]{:S(2)}) async-start(s8[23068672]{0:T(1024)(128)(4,1)} %bitcast.19), calls=%async_computation.9 | async-start | bytes 4194304
  102.6 256.8 %all-to-all-start = ((bf16[16,256,1408]{1,0,2:T(8,128)(2,1)}), bf16[16,256,1408]{1,0,2:T(8,128)(2,1)}, u32[]{:S(2)}, u32[]{:S(2)}) async-start(bf16[16,256,1408]{1,0,2:T(8,128)(2,1)} %divide_convert_fusion.1), calls=%async_computation | async-start | bytes 23068672 | tf_op jit(solution)/shard_map/all_to_all | solution.py:22
  108.0 23.7 %copy-start = (f32[16,1408]{1,0:T(8,128)S(1)}, f32[16,1408]{1,0:T(8,128)}, u32[]{:S(2)}) copy-start(f32[16,1408]{1,0:T(8,128)} %get-tuple-element.8) | copy-start | bytes 270340
  132.0 232.6 %copy-start.1 = (f32[16,1408]{1,0:T(8,128)S(1)}, f32[16,1408]{1,0:T(8,128)}, u32[]{:S(2)}) copy-start(f32[16,1408]{1,0:T(8,128)} %get-tuple-element.9) | copy-start | bytes 270340
  359.4 256.5 %all-to-all-start.1 = ((bf16[16,256,1408]{1,0,2:T(8,128)(2,1)}), bf16[16,256,1408]{1,0,2:T(8,128)(2,1)}, u32[]{:S(2)}, u32[]{:S(2)}) async-start(bf16[16,256,1408]{1,0,2:T(8,128)(2,1)} %divide_convert_fusion), calls=%async_computation.1 | async-start | bytes 23068672 | tf_op jit(solution)/shard_map/all_to_all | solution.py:23
  364.9 256.3 %copy-start.2 = (f32[256,16]{0,1:T(8,128)S(1)}, f32[256,16]{0,1:T(8,128)}, u32[]{:S(2)}) copy-start(f32[256,16]{0,1:T(8,128)} %param.8) | copy-start | bytes 49156
  364.9 256.3 %copy-start.3 = (f32[256]{0:T(256)S(1)}, f32[256]{0:T(256)}, u32[]{:S(2)}) copy-start(f32[256]{0:T(256)} %param.9) | copy-start | bytes 3076
  615.9 332.5 %all-to-all-start.2 = ((bf16[16,1408,256]{2,0,1:T(8,128)(2,1)}), bf16[16,1408,256]{2,0,1:T(8,128)(2,1)}, u32[]{:S(2)}, u32[]{:S(2)}) async-start(bf16[16,1408,256]{2,0,1:T(8,128)(2,1)} %fusion), calls=%async_computation.2 | async-start | bytes 23068672 | tf_op jit(solution)/shard_map/all_to_all | solution.py:25
Sparse Core Ops, SparseCore 0:
  31.1 56.0 all-reduce.2
where the time goes:
time: 988 us; the launch traced here: 985 us
  waiting for transfers between devices  464 us (47%)
  blocking collectives  266 us (27%)
  local copies, waits for them, and re-layouts  140 us (14%)
  other arithmetic  84.8 us (9%)
  starting transfers between devices  16 us (2%)
  between operations  14.2 us (1%)
    all_gather x1, blocking collectives, per_device(): row_router = lax.all_gather(part_router, 'fsdp', axis=0, tiled=True)  257 us
    all_to_all x1, waiting for transfers between devices, per_device(): lax.all_to_all(narrow_up, 'fsdp', split_axis=2, concat_axis=1, tiled=True)  218 us
    all_to_all x1, waiting for transfers between devices, per_device(): lax.all_to_all(narrow_gate, 'fsdp', split_axis=2, concat_axis=1, tiled=True)  213 us
    unnamed x23, local copies, waits for them, and re-layouts  48.2 us
    convert_element_type x1, other arithmetic, per_device(): (train_down / jnp.expand_dims(scale_down, 2)).astype(jnp.bfloat16)  32.6 us
    pmax x1, waiting for transfers between devices, per_device(): lax.pmax((jnp.max(jnp.abs(train_gate), axis=1), jnp.max(jnp.abs(train_up)...  32.5 us
    all_to_all x2, local copies, waits for them, and re-layouts, per_device(): lax.all_to_all(narrow_down, 'fsdp', split_axis=1, concat_axis=2, tiled=True)  29.3 us
    all_to_all x2, local copies, waits for them, and re-layouts, per_device(): lax.all_to_all(narrow_gate, 'fsdp', split_axis=2, concat_axis=1, tiled=True)  29.3 us
  transfers between devices with their start and end apart: 4, of which 3 were waited for; matrix products, arithmetic and copies ran while one was open for 12% of the time, Pallas kernels for 0%

commit v1 on v0

--- a/solution.py
+++ b/solution.py
@@ -2,6 +2,10 @@
 import jax.numpy as jnp
 from jax import lax
 from jax.sharding import PartitionSpec as P
+
+
+def after(value, earlier):
+    return lax.optimization_barrier((value, earlier))[0]
 
 
 def per_device(train_gate, train_up, train_down, router_weight, router_gain):
@@ -22,7 +26,7 @@
         lax.all_to_all(narrow_gate, "fsdp", split_axis=2, concat_axis=1, tiled=True),
         lax.all_to_all(narrow_up, "fsdp", split_axis=2, concat_axis=1, tiled=True),
     )
-    ready_down = lax.all_to_all(narrow_down, "fsdp", split_axis=1, concat_axis=2, tiled=True)
+    ready_down = lax.all_to_all(after(narrow_down, ready_gate), "fsdp", split_axis=1, concat_axis=2, tiled=True)
     scale_gate = lax.dynamic_slice_in_dim(
         scale_gate, lax.axis_index("fsdp") * ready_gate.shape[2], ready_gate.shape[2], axis=1
     )
@@ -33,8 +37,8 @@
         scale_down, lax.axis_index("fsdp") * ready_down.shape[1], ready_down.shape[1], axis=1
     )
     part_router = (router_weight * router_gain[:, None]).astype(jnp.bfloat16)
-    row_router = lax.all_gather(part_router, "fsdp", axis=0, tiled=True)
-    serve_router = lax.all_gather(row_router, "ep", axis=1, tiled=True)
+    wide_router = lax.all_gather(after(part_router, ready_up), "ep", axis=1, tiled=True)
+    serve_router = lax.all_gather(wide_router, "fsdp", axis=0, tiled=True)
     return (ready_gate, ready_up, ready_down, scale_gate, scale_up, scale_down, serve_router)
 
 

time: 988 us -> 921 us (0.932)
  blocking collectives: 266 us -> 226 us
  waiting for transfers between devices: 464 us -> 435 us
    all_gather x2, blocking collectives: 266 us -> 226 us  [the longest x1 218 us: per_device(): serve_router = lax.all_gather(wide_router, 'fsdp', axis=0, tiled=True)]
    all_to_all x1, waiting for transfers between devices: 218 us -> 189 us  [per_device(): lax.all_to_all(narrow_up, 'fsdp', split_axis=2, concat_axis=1, tiled=True)]
    unnamed x23 -> x13, local copies, waits for them, and re-layouts: 48.2 us -> 52.8 us
  transfers between devices with their start and end apart: 4 -> 4, of which waited for: 3 -> 3; matrix products, arithmetic and copies ran while one was open for 12% -> 13% of each run, Pallas kernels for 0% -> 0%
where the time goes in v1:
time: 921 us; the launch traced here: 918 us
  waiting for transfers between devices  435 us (47%)
  blocking collectives  226 us (25%)
  local copies, waits for them, and re-layouts  144 us (16%)
  other arithmetic  82.1 us (9%)
  starting transfers between devices  16.2 us (2%)
  between operations  14.1 us (2%)
    all_gather x1, blocking collectives, per_device(): serve_router = lax.all_gather(wide_router, 'fsdp', axis=0, tiled=True)  218 us
    all_to_all x1, waiting for transfers between devices, per_device(): lax.all_to_all(narrow_gate, 'fsdp', split_axis=2, concat_axis=1, tiled=True)  213 us
    all_to_all x1, waiting for transfers between devices, per_device(): lax.all_to_all(narrow_up, 'fsdp', split_axis=2, concat_axis=1, tiled=True)  189 us
    unnamed x13, local copies, waits for them, and re-layouts  52.8 us
    convert_element_type x1, other arithmetic, per_device(): (train_down / jnp.expand_dims(scale_down, 2)).astype(jnp.bfloat16)  32.6 us
    pmax x1, waiting for transfers between devices, per_device(): lax.pmax((jnp.max(jnp.abs(train_gate), axis=1), jnp.max(jnp.abs(train_up)...  32.5 us
    all_to_all x2, local copies, waits for them, and re-layouts, per_device(): lax.all_to_all(narrow_gate, 'fsdp', split_axis=2, concat_axis=1, tiled=True)  29.3 us
    all_to_all x2, local copies, waits for them, and re-layouts, per_device(): lax.all_to_all(after(narrow_down, ready_gate), 'fsdp', split_axis=1, conc...  29.3 us
  transfers between devices with their start and end apart: 4, of which 3 were waited for; matrix products, arithmetic and copies ran while one was open for 13% of the time, Pallas kernels for 0%

profile of v1, /device:TPU:0, one launch (start us, length us, event | category | flops | bytes accessed | tf_op | source)
XLA Modules:
  0.0 918.1 jit_solution(15523169974277981195)
XLA Ops:
  7.2 9.7 %abs_reduce_fusion.2 = f32[16,1408]{1,0:T(8,128)} fusion(f32[16,256,1408]{2,1,0:T(8,128)} %param.5), kind=kLoop, calls=%fused_computation.6 | loop fusion | flops 11511808 | bytes 23158784 | tf_op jit(solution)/shard_map/reduce_max | solution.py:14
  16.9 4.5 copy-done
  21.4 2.4 abs_reduce_fusion.1
  23.8 9.0 abs_reduce_fusion
  32.9 23.8 %copy.24 = f32[16,256,1408]{1,0,2:T(8,128)} copy(f32[16,256,1408]{2,1,0:T(8,128)} %param.5) | data formatting | bytes 46137344 | tf_op args[0]
  56.6 32.5 %all-reduce.3.cloned.1.call-done = (f32[16,1408]{1,0:T(8,128)}, f32[16,1408]{1,0:T(8,128)}, f32[16,1408]{1,0:T(8,128)}) async-done(((f32[16,1408]{1,0:T(8,128)}, f32[16,1408]{1,0:T(8,128)}, f32[16,1408]{1,0:T(8,128)}), (f32[16,1408]{1,0:T(8,128)}, f32[16,1408]{1,0:T(8,128)}, f32[16,1408]{1,0:T(8,128)})) %all-reduce.3.cloned.1.call-update) | async-done | bytes 270352 | tf_op jit(solution)/shard_map/pmax | solution.py:12
  90.3 14.2 %divide_convert_fusion.1 = bf16[16,256,1408]{1,0,2:T(8,128)(2,1)} fusion(f32[16,256,1408]{1,0,2:T(8,128)} %copy.24, f32[16,1408]{0,1:T(8,128)S(1)} %copy.23), kind=kLoop, calls=%fused_computation.5 | loop fusion | flops 11534336 | bytes 34693120 | tf_op jit(solution)/shard_map/convert_element_type | solution.py:21
  104.5 5.4 all-to-all-start
  109.9 23.8 %copy.28 = f32[16,256,1408]{1,0,2:T(8,128)} copy(f32[16,256,1408]{2,1,0:T(8,128)} %param.6) | data formatting | bytes 46137344 | tf_op args[1]
  133.9 14.2 %divide_convert_fusion = bf16[16,256,1408]{1,0,2:T(8,128)(2,1)} fusion(f32[16,256,1408]{1,0,2:T(8,128)} %copy.28, f32[16,1408]{0,1:T(8,128)S(1)} %copy.27), kind=kLoop, calls=%fused_computation.3 | loop fusion | flops 11534336 | bytes 34693120 | tf_op jit(solution)/shard_map/convert_element_type | solution.py:22
  148.2 213.1 %all-to-all-done = bf16[16,256,1408]{1,0,2:T(8,128)(2,1)} async-done(((bf16[16,256,1408]{1,0,2:T(8,128)(2,1)}), bf16[16,256,1408]{1,0,2:T(8,128)(2,1)}, u32[]{:S(2)}, u32[]{:S(2)}) %all-to-all-start) | async-done | bytes 11534368 | tf_op jit(solution)/shard_map/all_to_all | solution.py:26
  361.3 5.3 all-to-all-start.1
  366.8 32.6 %fusion = bf16[16,1408,256]{2,0,1:T(8,128)(2,1)} fusion(f32[16,1408,256]{2,1,0:T(8,128)} %param.7, f32[16,1408]{0,1:T(8,128)S(1)} %copy.31), kind=kLoop, calls=%fused_computation.1 | loop fusion | flops 11534336 | bytes 34693120 | tf_op jit(solution)/shard_map/convert_element_type | solution.py:23
  399.4 11.3 %copy.26 = bf16[16,8,256,176]{2,1,3,0:T(8,128)(2,1)} copy(bf16[16,8,256,176]{2,0,3,1:T(8,128)(2,1)} %bitcast.2) | data formatting | bytes 23068672 | tf_op jit(solution)/shard_map/all_to_all | solution.py:26
  410.7 18.0 %all_to_all.42 = bf16[16,2048,176]{1,2,0:T(8,128)(2,1)} reshape(bf16[16,8,256,176]{2,1,3,0:T(8,128)(2,1)} %copy.26) | data formatting | bytes 23068672 | tf_op jit(solution)/shard_map/all_to_all | solution.py:26
  428.7 189.1 %all-to-all-done.1 = bf16[16,256,1408]{1,0,2:T(8,128)(2,1)} async-done(((bf16[16,256,1408]{1,0,2:T(8,128)(2,1)}), bf16[16,256,1408]{1,0,2:T(8,128)(2,1)}, u32[]{:S(2)}, u32[]{:S(2)}) %all-to-all-start.1) | async-done | bytes 11534368 | tf_op jit(solution)/shard_map/all_to_all | solution.py:27
  617.8 5.4 all-to-all-start.2
  623.3 1.4 constant_dynamic-slice_fusion.2
  625.4 11.3 %copy.30 = bf16[16,8,256,176]{2,1,3,0:T(8,128)(2,1)} copy(bf16[16,8,256,176]{2,0,3,1:T(8,128)(2,1)} %bitcast.5) | data formatting | bytes 23068672 | tf_op jit(solution)/shard_map/all_to_all | solution.py:27
  636.8 18.0 %all_to_all.46 = bf16[16,2048,176]{1,2,0:T(8,128)(2,1)} reshape(bf16[16,8,256,176]{2,1,3,0:T(8,128)(2,1)} %copy.30) | data formatting | bytes 23068672 | tf_op jit(solution)/shard_map/all_to_all | solution.py:27
  654.7 8.1 all_gather.6
  662.9 218.3 %all_gather.7 = bf16[2048,64]{0,1:T(8,128)(2,1)S(1)} all-gather(bf16[256,64]{0,1:T(8,128)(2,1)S(1)} %all_gather.6), channel_id=1, replica_groups=mesh['ep'=4,'fsdp'=8] {'fsdp'}, dimensions={0}, use_global_device_ids=true | all-gather | bytes 294912 | tf_op jit(solution)/shard_map/all_gather | solution.py:41
  881.2 11.4 %copy.33 = bf16[16,176,8,256]{3,2,1,0:T(8,128)(2,1)} copy(bf16[16,176,8,256]{3,0,1,2:T(8,128)(2,1)} %bitcast.7) | data formatting | bytes 23068672 | tf_op jit(solution)/shard_map/all_to_all | solution.py:29
  892.6 18.0 %all_to_all.50 = bf16[16,176,2048]{2,1,0:T(8,128)(2,1)} reshape(bf16[16,176,8,256]{3,2,1,0:T(8,128)(2,1)} %copy.33) | data formatting | bytes 23068672 | tf_op jit(solution)/shard_map/all_to_all | solution.py:29
  (18 shorter events, 3.1 us)
Async XLA Ops:
  7.2 81.9 %all-reduce.3.cloned.1.call-start = ((), (), s32[]{:S(2)}) async-start(), calls=%async_computation.3 | async-start | bytes 540672 | tf_op jit(solution)/shard_map/pmax | solution.py:12
  7.2 14.2 %copy-start = (f32[16,256,1408]{2,1,0:T(8,128)S(1)}, f32[16,256,1408]{2,1,0:T(8,128)}, u32[]{:S(2)}) copy-start(f32[16,256,1408]{2,1,0:T(8,128)} %param.6) | copy-start | bytes 69206016
  104.5 256.8 %all-to-all-start = ((bf16[16,256,1408]{1,0,2:T(8,128)(2,1)}), bf16[16,256,1408]{1,0,2:T(8,128)(2,1)}, u32[]{:S(2)}, u32[]{:S(2)}) async-start(bf16[16,256,1408]{1,0,2:T(8,128)(2,1)} %divide_convert_fusion.1), calls=%async_computation | async-start | bytes 23068672 | tf_op jit(solution)/shard_map/all_to_all | solution.py:26
  109.9 23.8 %copy-start.1 = (f32[16,1408]{1,0:T(8,128)S(1)}, f32[16,1408]{1,0:T(8,128)}, u32[]{:S(2)}) copy-start(f32[16,1408]{1,0:T(8,128)} %get-tuple-element.12) | copy-start | bytes 270340
  133.9 232.7 %copy-start.2 = (f32[16,1408]{1,0:T(8,128)S(1)}, f32[16,1408]{1,0:T(8,128)}, u32[]{:S(2)}) copy-start(f32[16,1408]{1,0:T(8,128)} %get-tuple-element.13) | copy-start | bytes 270340
  361.3 256.6 %all-to-all-start.1 = ((bf16[16,256,1408]{1,0,2:T(8,128)(2,1)}), bf16[16,256,1408]{1,0,2:T(8,128)(2,1)}, u32[]{:S(2)}, u32[]{:S(2)}) async-start(bf16[16,256,1408]{1,0,2:T(8,128)(2,1)} %divide_convert_fusion), calls=%async_computation.1 | async-start | bytes 23068672 | tf_op jit(solution)/shard_map/all_to_all | solution.py:27
  410.7 212.6 %copy-start.3 = (f32[256,16]{0,1:T(8,128)S(1)}, f32[256,16]{0,1:T(8,128)}, u32[]{:S(2)}) copy-start(f32[256,16]{0,1:T(8,128)} %param.8) | copy-start | bytes 49156
  410.7 212.6 %copy-start.4 = (f32[256]{0:T(256)S(1)}, f32[256]{0:T(256)}, u32[]{:S(2)}) copy-start(f32[256]{0:T(256)} %param.9) | copy-start | bytes 3076
  617.8 263.4 %all-to-all-start.2 = ((bf16[16,1408,256]{2,0,1:T(8,128)(2,1)}), bf16[16,1408,256]{2,0,1:T(8,128)(2,1)}, u32[]{:S(2)}, u32[]{:S(2)}) async-start(bf16[16,1408,256]{2,0,1:T(8,128)(2,1)} %fusion), calls=%async_computation.2 | async-start | bytes 23068672 | tf_op jit(solution)/shard_map/all_to_all | solution.py:29
Sparse Core Ops, SparseCore 0:
  33.0 56.0 all-reduce.2
